TPU v7x, 1024 devices: a whole 4x4x32 slice. The times are simulated.
1024 devices in a mesh: dp: 16 (over y_lo, x, core), mp: 64 (over z, y_hi).
Axes of the slice: x: 4, y: 4 (y_hi: 2, y_lo: 2; y = y_hi * 2 + y_lo), z: 32, core: 2. Of those that a mesh axis runs over, the one named last changes fastest.
Arguments:
- cotangent: bfloat16 [2048, 4608], P(('dp', 'mp')), may hold values from -50 to 50
- mlp_out: bfloat16 [2048, 4608], P(('dp', 'mp')), may hold values from -500 to 500
- post_gain: float32 [4608], replicated, may hold values from 0.5 to 1.5
- down_weight: bfloat16 [36864, 4608], P('mp', 'dp'), may hold values from -0.09375 to 0.09375
- gate_pre: bfloat16 [2048, 36864], P('dp', 'mp'), may hold values from -6 to 6
- up_pre: bfloat16 [2048, 36864], P('dp', 'mp'), may hold values from -6 to 6
Outputs:
- gate_grad: float32 [2048, 36864], P('dp', 'mp')
- up_grad: float32 [2048, 36864], P('dp', 'mp')
- gain_grad: float32 [4608], replicated
All inputs are finite; a program needn't handle non-finite values.
Results may differ from a plain program's by a relative error of at most 0.0005.
Values may be sent and summed in bfloat16 or wider, within the bound.
No kernel may reach another device: no remote copies, remote signals or barrier semaphores. Data moves between devices by JAX's collectives and lax.ppermute only.
A program may use at most 32 MiB of HBM per device.

v0:
```python
import jax
import jax.numpy as jnp
from jax import lax
from jax.experimental import pallas as pl
from jax.experimental.pallas import tpu as pltpu
from jax.sharding import Mesh
from jax.sharding import PartitionSpec as P


D = 4608
DP = ("yl", "x", "c")
MP = ("z", "yh")
ALL = DP + MP
PLANE = ("yl", "x", "c", "yh")
epsilon = 1e-06

LANES = 128
KT = D // LANES
ROWS = 80
GROWS = 80
Z = 32
LOW = 256.0


def pre_kernel(c_ref, y_ref, g_ref, m_ref):
    y = y_ref[...].astype(jnp.float32)
    c = c_ref[...].astype(jnp.float32)
    gain = jnp.broadcast_to(g_ref[...].reshape(1, D), (1, D))
    rm = jnp.sqrt(jnp.sum(y * y, axis=1, keepdims=True) / D + epsilon)
    gp = jnp.sum(c * (y / rm), axis=0, keepdims=True)
    scaled = c * gain
    ps = jnp.sum(scaled * y, axis=1, keepdims=True)
    og = scaled / rm - y * (ps / (D * (rm * rm * rm)))
    top = jnp.max(jnp.abs(og), axis=1, keepdims=True)
    e = jnp.clip(jnp.ceil(jnp.log2(jnp.maximum(top, 1e-37))), -100.0, 100.0)
    q = og * jnp.exp2(-e)
    gtop = jnp.max(jnp.abs(gp), axis=1, keepdims=True)
    ge = jnp.clip(jnp.ceil(jnp.log2(jnp.maximum(gtop, 1e-37))), -100.0, 100.0)
    gx = gp * jnp.exp2(-ge)
    hi = gx.astype(jnp.bfloat16).astype(jnp.float32)
    lo = (gx - hi) * LOW
    for k in range(KT):
        m_ref[2 * k : 2 * k + 2, :] = q[:, LANES * k : LANES * (k + 1)]
        m_ref[ROWS + k : ROWS + k + 1, :] = hi[:, LANES * k : LANES * (k + 1)]
        m_ref[ROWS + KT + k : ROWS + KT + k + 1, :] = lo[:, LANES * k : LANES * (k + 1)]
    m_ref[2 * KT : 2 * KT + 2, :] = jnp.broadcast_to(e, (2, LANES))
    m_ref[2 * KT + 2 : ROWS, :] = jnp.zeros((ROWS - 2 * KT - 2, LANES), jnp.float32)
    m_ref[ROWS + 2 * KT : ROWS + 2 * KT + 1, :] = jnp.broadcast_to(ge, (1, LANES))
    m_ref[ROWS + 2 * KT + 1 :, :] = jnp.zeros((GROWS - 2 * KT - 1, LANES), jnp.float32)


KSTEP = 12
NSTEP = KT // KSTEP


def products(src_ref, w_ref, acc_ref):
    step = pl.program_id(0)

    @pl.when(step == 0)
    def _():
        acc_ref[...] = jnp.zeros_like(acc_ref)

    scales = [jnp.exp2(src_ref[pl.ds(2 * KT + r, Z, stride=ROWS), :]) for r in range(2)]
    his, los = [], []
    for kk in range(KSTEP):
        x = jnp.concatenate(
            [src_ref[pl.ds(2 * (step * KSTEP + kk) + r, Z, stride=ROWS), :] * scales[r] for r in range(2)], axis=0
        )
        hi = x.astype(jnp.bfloat16)
        his.append(hi)
        los.append((x - hi.astype(jnp.float32)).astype(jnp.bfloat16))
    x_all = jnp.concatenate([jnp.concatenate(his, axis=1), jnp.concatenate(los, axis=1)], axis=0)
    acc_ref[...] += jnp.dot(x_all, w_ref[...], preferred_element_type=jnp.float32)


def own_kernel(own_ref, w_ref, out_ref, acc_ref):
    products(own_ref, w_ref, acc_ref)

    @pl.when(pl.program_id(0) == NSTEP - 1)
    def _():
        out_ref[...] = acc_ref[: 2 * Z, :] + acc_ref[2 * Z :, :]


def last_kernel(yh_ref, rec_ref, w_ref, own_ref, gate_ref, up_ref, gg_ref, ug_ref, acc_ref, nat_ref):
    products(rec_ref, w_ref, acc_ref)

    @pl.when(pl.program_id(0) == NSTEP - 1)
    def _():
        n = acc_ref.shape[1]
        yh = yh_ref[0]
        halves = (own_ref[...], acc_ref[: 2 * Z, :] + acc_ref[2 * Z :, :])
        for j in range(0, n, LANES):
            w = min(LANES, n - j)
            for h in range(2):
                at = yh if h == 0 else 1 - yh
                for r in range(2):
                    part = halves[h][r * Z : (r + 1) * Z, j : j + w]
                    if w < LANES:
                        part = jnp.concatenate([part, jnp.zeros((Z, LANES - w), jnp.float32)], axis=1)
                    nat_ref[j // LANES, pl.ds(at * 2 + r, Z, stride=4), :] = part
            hidden = nat_ref[j // LANES].T[:w]
            g = gate_ref[j : j + w, :].astype(jnp.float32)
            u = up_ref[j : j + w, :].astype(jnp.float32)
            k0 = 0.7978845608028654
            g2 = g * g
            t = jnp.tanh(k0 * (g + 0.044715 * (g2 * g)))
            half = 0.5 * (1.0 + t)
            slope = half + (0.5 * k0) * g * (1.0 - t * t) * (1.0 + (3 * 0.044715) * g2)
            gg_ref[j : j + w, :] = hidden * u * slope
            ug_ref[j : j + w, :] = hidden * (g * half)


def whole(*shape):
    return pl.BlockSpec(shape, lambda i: (0,) * len(shape))


def run_own(own, weight, interpret=False):
    n = weight.shape[1]
    return pl.pallas_call(
        own_kernel,
        grid=(NSTEP,),
        in_specs=[whole(Z * ROWS, LANES), pl.BlockSpec((KSTEP * LANES, n), lambda i: (i, 0))],
        out_specs=whole(2 * Z, n),
        out_shape=jax.ShapeDtypeStruct((2 * Z, n), jnp.float32),
        scratch_shapes=[pltpu.VMEM((4 * Z, n), jnp.float32)],
        cost_estimate=pl.CostEstimate(flops=4 * 2 * Z * n * D, transcendentals=0, bytes_accessed=2 * n * D),
        name="own",
        interpret=interpret,
    )(own, weight)


def run_last(yh, rec, weight, own, gate, up, interpret=False):
    n, rows = gate.shape
    shape = jax.ShapeDtypeStruct((n, rows), jnp.float32)
    return pl.pallas_call(
        last_kernel,
        grid=(NSTEP,),
        in_specs=[
            pl.BlockSpec(memory_space=pltpu.SMEM),
            whole(Z * ROWS, LANES),
            pl.BlockSpec((KSTEP * LANES, n), lambda i: (i, 0)),
            whole(2 * Z, n),
            whole(n, rows),
            whole(n, rows),
        ],
        out_specs=[whole(n, rows), whole(n, rows)],
        out_shape=(shape, shape),
        scratch_shapes=[
            pltpu.VMEM((4 * Z, n), jnp.float32),
            pltpu.VMEM(((n + LANES - 1) // LANES, rows, LANES), jnp.float32),
        ],
        name="last",
        interpret=interpret,
    )(yh, rec, weight, own, gate, up)


def spread(v, axes):
    n = lax.axis_size(axes)
    return lax.all_to_all(jnp.broadcast_to(v[None], (n,) + v.shape), axes, 0, 0, tiled=True)


def steps(cotangent, mlp_out, post_gain, down_weight, gate_pre, up_pre):
    weight = lax.all_gather(down_weight.T, DP, axis=0, tiled=True)
    message = pl.pallas_call(
        pre_kernel,
        out_shape=jax.ShapeDtypeStruct((ROWS + GROWS, LANES), jnp.float32),
        name="pre",
    )(cotangent, mlp_out, post_gain)
    got = lax.all_gather(message.astype(jnp.float16), "z", axis=0)
    own = got[:, :ROWS].reshape(Z * ROWS, LANES)
    other = lax.ppermute(own, "yh", [(0, 1), (1, 0)])
    terms = got[:, ROWS:].astype(jnp.float32)
    gain = jnp.sum(
        (terms[:, :KT] + terms[:, KT : 2 * KT] * (1.0 / LOW)) * jnp.exp2(terms[:, 2 * KT : 2 * KT + 1]), axis=0
    )
    parts = spread(gain, PLANE)
    gain_grad = jnp.sum(parts, axis=0).reshape(D)
    hidden = run_own(own.astype(jnp.float32), weight)
    gate_grad, up_grad = run_last(
        lax.axis_index("yh").reshape(1), other.astype(jnp.float32), weight, hidden, gate_pre.T, up_pre.T
    )
    return (gate_grad.T, up_grad.T, gain_grad)


def solution(mesh):
    finer = Mesh(mesh.devices.reshape(2, 4, 2, Z, 2), ALL)
    in_specs = (P(ALL, None), P(ALL, None), P(), P(MP, DP), P(DP, MP), P(DP, MP))
    out_specs = (P(DP, MP), P(DP, MP), P())
    return jax.shard_map(steps, mesh=finer, in_specs=in_specs, out_specs=out_specs, check_vma=False)
```

profile of v0, /device:TPU:1, one launch (start us, length us, event | category | flops | bytes accessed | tf_op | source)
XLA Modules:
  0.0 140.7 jit_solution(241940242820305945)
XLA Ops:
  7.2 0.0 all-gather.4.cloned.1.call-start
  7.2 0.7 all-gather.4.cloned.1.call-update
  7.9 1.7 %pre.1 = f32[160,128]{1,0:T(8,128)} custom-call(bf16[2,4608]{1,0:T(2,128)(2,1)} %c_ref.1, bf16[2,4608]{1,0:T(2,128)(2,1)} %y_ref.1, f32[4608]{0:T(1024)} %g_ref.1), custom_call_target="tpu_custom_call" | custom-call | tf_op jit(solution)/shard_map/pre/pallas_call | solution.py:164
  9.6 0.9 convert_element_type.12
  10.5 63.2 %all-gather.5 = f16[5120,128]{1,0:T(8,128)(2,1)S(1)} all-gather(f16[160,128]{1,0:T(8,128)(2,1)S(1)} %convert_element_type.12), channel_id=2, replica_groups=mesh['yl'=2,'x'=4,'c'=2,'z'=32,'yh'=2] {'z'}, dimensions={0}, use_global_device_ids=true | all-gather | bytes 1351680 | tf_op jit(solution)/shard_map/all_gather | solution.py:169
  73.7 0.2 slice_convert_fusion
  74.0 0.2 fusion.2
  74.2 0.9 broadcast_in_dim.2
  75.1 21.0 %all-to-all-start = ((f32[32,36,128]{2,1,0:T(8,128)}), f32[32,36,128]{2,1,0:T(8,128)S(1)}, u32[]{:S(2)}, u32[]{:S(2)}) async-start(f32[32,36,128]{2,1,0:T(8,128)} %broadcast_in_dim.2), calls=%async_computation | async-start | bytes 1310720 | tf_op jit(solution)/shard_map/all_to_all | solution.py:159
  96.1 4.8 %collective-permute-start = (f16[2560,128]{1,0:T(8,128)(2,1)S(1)}, f16[2560,128]{1,0:T(8,128)(2,1)S(1)}, u32[]{:S(2)}, u32[]{:S(2)}) collective-permute-start(f16[2560,128]{1,0:T(8,128)(2,1)S(1)} %bitcast.12), channel_id=1, source_target_pairs={{0,1},{1,0},{2,3},{3,2},{4,5},{5,4},{6,7},{7,6},{8,9},{9,8},{10,11... | collective-permute-start | bytes 1966088 | tf_op jit(solution)/shard_map/ppermute | solution.py:171
  100.9 1.2 bitcast_convert_fusion.own_ref
  102.1 7.2 %all-to-all-done = f32[32,36,128]{2,1,0:T(8,128)S(1)} async-done(((f32[32,36,128]{2,1,0:T(8,128)}), f32[32,36,128]{2,1,0:T(8,128)S(1)}, u32[]{:S(2)}, u32[]{:S(2)}) %all-to-all-start) | async-done | bytes 589856 | tf_op jit(solution)/shard_map/all_to_all | solution.py:159
  109.3 0.7 reduce_sum.19
  109.9 11.8 %collective-permute-done = f16[2560,128]{1,0:T(8,128)(2,1)S(1)} collective-permute-done((f16[2560,128]{1,0:T(8,128)(2,1)S(1)}, f16[2560,128]{1,0:T(8,128)(2,1)S(1)}, u32[]{:S(2)}, u32[]{:S(2)}) %collective-permute-start) | collective-permute-done | bytes 655392 | tf_op jit(solution)/shard_map/ppermute | solution.py:171
  121.8 1.2 convert_element_type.13.rec_ref
  122.9 0.0 all-gather.4.cloned.1.call-done.w_ref
  122.9 5.2 %own.1.own_ref = f32[64,576]{1,0:T(8,128)} custom-call(f32[2560,128]{1,0:T(8,128)} %bitcast_convert_fusion.own_ref, bf16[4608,576]{1,0:T(8,128)(2,1)} %all-gather.4.cloned.1.call-done.w_ref), custom_call_target="tpu_custom_call" | custom-call | flops 679477248 | bytes 5308416 | tf_op jit(solution)/shard_map/own/pallas_call | solution.py:119
  128.2 5.7 %last.1 = (f32[576,128]{1,0:T(8,128)}, f32[576,128]{1,0:T(8,128)}) custom-call(s32[1]{0:T(128)} %bitcast.yh_ref, f32[2560,128]{1,0:T(8,128)} %convert_element_type.13.rec_ref, bf16[4608,576]{1,0:T(8,128)(2,1)} %all-gather.4.cloned.1.call-done.w_ref, f32[64,576]{1,0:T(8,128)} %own.1.own_ref, bf16[576,128]{1,0:T(8,128)(2,1)} %bitcast.14, bf16[576,128]{1,0:T(8,128)(2,1)} %bitcast.15), custom_call_target="tpu_custom_call" | custom-call | tf_op jit(solution)/shard_map/last/pallas_call | solution.py:135
  (1 shorter events, 0.0 us)
Async XLA Ops:
  7.2 115.8 %all-gather.4.cloned.1.call-start = ((), (), s32[]{:S(2)}) async-start(), calls=%async_computation.1 | async-start | bytes 6266880 | tf_op jit(solution)/shard_map/all_gather | solution.py:163
  75.1 34.2 %all-to-all-start = ((f32[32,36,128]{2,1,0:T(8,128)}), f32[32,36,128]{2,1,0:T(8,128)S(1)}, u32[]{:S(2)}, u32[]{:S(2)}) async-start(f32[32,36,128]{2,1,0:T(8,128)} %broadcast_in_dim.2), calls=%async_computation | async-start | bytes 1310720 | tf_op jit(solution)/shard_map/all_to_all | solution.py:159
  96.1 25.7 %collective-permute-start = (f16[2560,128]{1,0:T(8,128)(2,1)S(1)}, f16[2560,128]{1,0:T(8,128)(2,1)S(1)}, u32[]{:S(2)}, u32[]{:S(2)}) collective-permute-start(f16[2560,128]{1,0:T(8,128)(2,1)S(1)} %bitcast.12), channel_id=1, source_target_pairs={{0,1},{1,0},{2,3},{3,2},{4,5},{5,4},{6,7},{7,6},{8,9},{9,8},{10,11... | collective-permute-start | bytes 1966088 | tf_op jit(solution)/shard_map/ppermute | solution.py:171
Sparse Core Ops, SparseCore 0:
  10.7 68.1 all-gather.3
where the time goes:
time: 141 us
  blocking collectives  63.2 us (45%)
  starting transfers between devices  25.8 us (18%)
  waiting for transfers between devices  19.7 us (14%)
  between operations  14.1 us (10%)
  Pallas kernels  12.7 us (9%)
  other arithmetic  4.36 us (3%)
    all_gather x1, blocking collectives, steps(): got = lax.all_gather(message.astype(jnp.float16), 'z', axis=0)  63.2 us
    all_to_all x1, starting transfers between devices, spread(): lax.all_to_all(jnp.broadcast_to(v[None], (n,) + v.shape), axes, 0, 0, til...  21 us
    ppermute x1, waiting for transfers between devices, steps(): other = lax.ppermute(own, 'yh', [(0, 1), (1, 0)])  11.8 us
    all_to_all x1, waiting for transfers between devices, spread(): lax.all_to_all(jnp.broadcast_to(v[None], (n,) + v.shape), axes, 0, 0, til...  7.17 us
    pallas_call x1, Pallas kernels, run_last(): pl.pallas_call(last_kernel, grid=(NSTEP,), in_specs=[pl.BlockSpec(memory_...  5.73 us
    pallas_call x1, Pallas kernels, run_own(): pl.pallas_call(own_kernel, grid=(NSTEP,), in_specs=[whole(Z * ROWS, LANES...  5.23 us
    ppermute x1, starting transfers between devices, steps(): other = lax.ppermute(own, 'yh', [(0, 1), (1, 0)])  4.76 us
  transfers between devices with their start and end apart: 3, of which 2 were waited for; matrix products, arithmetic and copies ran while one was open for 4% of the time, Pallas kernels for 1%

commit v1 on v0

v1 whole, which is shorter than its diff:
```python
import jax
import jax.numpy as jnp
from jax import lax
from jax.experimental import pallas as pl
from jax.experimental.pallas import tpu as pltpu
from jax.sharding import Mesh
from jax.sharding import PartitionSpec as P


D = 4608
DP = ("yl", "x", "c")
MP = ("z", "yh")
ALL = DP + MP
PLANE = ("yl", "x", "c", "yh")
epsilon = 1e-06

LANES = 128
KT = D // LANES
ROWS = 80
GROWS = 80
Z = 32
LOW = 256.0
VMEM = 20 << 20
STAGE_VMEM = 46 << 20


def pre_kernel(c_hbm, y_hbm, g_hbm, m_ref, c_ref, y_ref, g_ref, sems):
    pairs = ((c_hbm, c_ref), (y_hbm, y_ref), (g_hbm, g_ref))
    copies = [pltpu.make_async_copy(src, dst, sems.at[i]) for i, (src, dst) in enumerate(pairs)]
    for copy in copies:
        copy.start()
    for copy in copies:
        copy.wait()
    y = y_ref[...].astype(jnp.float32)
    c = c_ref[...].astype(jnp.float32)
    gain = jnp.broadcast_to(g_ref[...].reshape(1, D), (1, D))
    rm = jnp.sqrt(jnp.sum(y * y, axis=1, keepdims=True) / D + epsilon)
    gp = jnp.sum(c * (y / rm), axis=0, keepdims=True)
    scaled = c * gain
    ps = jnp.sum(scaled * y, axis=1, keepdims=True)
    og = scaled / rm - y * (ps / (D * (rm * rm * rm)))
    top = jnp.max(jnp.abs(og), axis=1, keepdims=True)
    e = jnp.clip(jnp.ceil(jnp.log2(jnp.maximum(top, 1e-37))), -100.0, 100.0)
    q = og * jnp.exp2(-e)
    gtop = jnp.max(jnp.abs(gp), axis=1, keepdims=True)
    ge = jnp.clip(jnp.ceil(jnp.log2(jnp.maximum(gtop, 1e-37))), -100.0, 100.0)
    gx = gp * jnp.exp2(-ge)
    hi = gx.astype(jnp.bfloat16).astype(jnp.float32)
    lo = (gx - hi) * LOW
    for k in range(KT):
        m_ref[2 * k : 2 * k + 2, :] = q[:, LANES * k : LANES * (k + 1)]
        m_ref[ROWS + k : ROWS + k + 1, :] = hi[:, LANES * k : LANES * (k + 1)]
        m_ref[ROWS + KT + k : ROWS + KT + k + 1, :] = lo[:, LANES * k : LANES * (k + 1)]
    m_ref[2 * KT : 2 * KT + 2, :] = jnp.broadcast_to(e, (2, LANES))
    m_ref[2 * KT + 2 : ROWS, :] = jnp.zeros((ROWS - 2 * KT - 2, LANES), jnp.float32)
    m_ref[ROWS + 2 * KT : ROWS + 2 * KT + 1, :] = jnp.broadcast_to(ge, (1, LANES))
    m_ref[ROWS + 2 * KT + 1 :, :] = jnp.zeros((GROWS - 2 * KT - 1, LANES), jnp.float32)


KSTEP = 12
NSTEP = KT // KSTEP


def parts(src_ref, step):
    scales = [jnp.exp2(src_ref[pl.ds(2 * KT + r, Z, stride=ROWS), :]) for r in range(2)]
    his, los = [], []
    for kk in range(KSTEP):
        x = jnp.concatenate(
            [src_ref[pl.ds(2 * (step * KSTEP + kk) + r, Z, stride=ROWS), :] * scales[r] for r in range(2)], axis=0
        )
        hi = x.astype(jnp.bfloat16)
        his.append(hi)
        los.append((x - hi.astype(jnp.float32)).astype(jnp.bfloat16))
    return jnp.concatenate([jnp.concatenate(his, axis=1), jnp.concatenate(los, axis=1)], axis=0)


def factor_kernel(w_hbm, gate_ref, up_ref, w_out, ga_ref, ua_ref, sem):
    copy = pltpu.make_async_copy(w_hbm, w_out, sem)
    copy.start()
    g = gate_ref[...].astype(jnp.float32)
    u = up_ref[...].astype(jnp.float32)
    k0 = 0.7978845608028654
    g2 = g * g
    t = jnp.tanh(k0 * (g + 0.044715 * (g2 * g)))
    half = 0.5 * (1.0 + t)
    ga_ref[...] = u * (half + (0.5 * k0) * g * (1.0 - t * t) * (1.0 + (3 * 0.044715) * g2))
    ua_ref[...] = g * half
    copy.wait()


def main_kernel(yh_ref, own_ref, rec_ref, w_ref, ga_ref, ua_ref, gg_ref, ug_ref, acc_ref, nat_ref):
    step = pl.program_id(0)

    @pl.when(step == 0)
    def _():
        acc_ref[...] = jnp.zeros_like(acc_ref)

    x_all = jnp.concatenate([parts(own_ref, step), parts(rec_ref, step)], axis=0)
    acc_ref[...] += jnp.dot(x_all, w_ref[...], preferred_element_type=jnp.float32)

    @pl.when(step == NSTEP - 1)
    def _():
        n = acc_ref.shape[1]
        yh = yh_ref[0]
        for j in range(0, n, LANES):
            w = min(LANES, n - j)
            for h in range(2):
                at = yh if h == 0 else 1 - yh
                for r in range(2):
                    row = (4 * h + r) * Z
                    part = acc_ref[row : row + Z, j : j + w] + acc_ref[row + 2 * Z : row + 3 * Z, j : j + w]
                    if w < LANES:
                        part = jnp.concatenate([part, jnp.zeros((Z, LANES - w), jnp.float32)], axis=1)
                    nat_ref[j // LANES, pl.ds(at * 2 + r, Z, stride=4), :] = part
            hidden = nat_ref[j // LANES].T[:w]
            gg_ref[j : j + w, :] = hidden * ga_ref[j : j + w, :]
            ug_ref[j : j + w, :] = hidden * ua_ref[j : j + w, :]


def whole(*shape):
    return pl.BlockSpec(shape, lambda i: (0,) * len(shape))


def run_factors(weight, gate, up, interpret=False):
    shape = jax.ShapeDtypeStruct(gate.shape, jnp.float32)
    vmem = pl.BlockSpec(memory_space=pltpu.VMEM)
    return pl.pallas_call(
        factor_kernel,
        in_specs=[pl.BlockSpec(memory_space=pl.ANY), vmem, vmem],
        out_specs=(pl.BlockSpec(memory_space=pl.ANY), vmem, vmem),
        out_shape=(jax.ShapeDtypeStruct(weight.shape, weight.dtype), shape, shape),
        scratch_shapes=[pltpu.SemaphoreType.DMA],
        cost_estimate=pl.CostEstimate(
            flops=20 * gate.size, transcendentals=gate.size, bytes_accessed=12 * gate.size + 4 * weight.size
        ),
        compiler_params=pltpu.CompilerParams(vmem_limit_bytes=STAGE_VMEM),
        name="factors",
        interpret=interpret,
    )(weight, gate, up)


def run_main(yh, own, rec, weight, ga, ua, interpret=False):
    n, rows = ga.shape
    shape = jax.ShapeDtypeStruct((n, rows), jnp.float32)
    return pl.pallas_call(
        main_kernel,
        grid=(NSTEP,),
        in_specs=[
            pl.BlockSpec(memory_space=pltpu.SMEM),
            whole(Z * ROWS, LANES),
            whole(Z * ROWS, LANES),
            pl.BlockSpec((KSTEP * LANES, n), lambda i: (i, 0)),
            whole(n, rows),
            whole(n, rows),
        ],
        out_specs=[whole(n, rows), whole(n, rows)],
        out_shape=(shape, shape),
        scratch_shapes=[
            pltpu.VMEM((2 * rows, n), jnp.float32),
            pltpu.VMEM(((n + LANES - 1) // LANES, rows, LANES), jnp.float32),
        ],
        compiler_params=pltpu.CompilerParams(vmem_limit_bytes=VMEM),
        name="main",
        interpret=interpret,
    )(yh, own, rec, weight, ga, ua)


def spread(v, axes):
    n = lax.axis_size(axes)
    return lax.all_to_all(jnp.broadcast_to(v[None], (n,) + v.shape), axes, 0, 0, tiled=True)


def steps(cotangent, mlp_out, post_gain, down_weight, gate_pre, up_pre):
    weight = lax.all_gather(down_weight.T, DP, axis=0, tiled=True)
    message = pl.pallas_call(
        pre_kernel,
        in_specs=[pl.BlockSpec(memory_space=pltpu.HBM)] * 3,
        out_shape=jax.ShapeDtypeStruct((ROWS + GROWS, LANES), jnp.float32),
        scratch_shapes=[
            pltpu.VMEM(cotangent.shape, cotangent.dtype),
            pltpu.VMEM(mlp_out.shape, mlp_out.dtype),
            pltpu.VMEM(post_gain.shape, post_gain.dtype),
            pltpu.SemaphoreType.DMA((3,)),
        ],
        compiler_params=pltpu.CompilerParams(vmem_limit_bytes=VMEM),
        name="pre",
    )(cotangent, mlp_out, post_gain)
    got = lax.all_gather(message.astype(jnp.float16), "z", axis=0)
    own = got[:, :ROWS].reshape(Z * ROWS, LANES)
    other = lax.ppermute(own, "yh", [(0, 1), (1, 0)])
    terms = got[:, ROWS:].astype(jnp.float32)
    expo = terms[:, 2 * KT : 2 * KT + 1]
    top = jnp.max(expo, axis=0)
    line = jnp.sum((terms[:, :KT] + terms[:, KT : 2 * KT] * (1.0 / LOW)) * jnp.exp2(expo - top), axis=0)
    line = jnp.concatenate([line, jnp.broadcast_to(top, (4, LANES))], axis=0).astype(jnp.float16)
    lines = spread(line, PLANE).astype(jnp.float32)
    gain_grad = jnp.sum(lines[:, :KT] * jnp.exp2(lines[:, KT : KT + 1]), axis=0).reshape(D)
    staged, ga, ua = run_factors(weight, gate_pre.T, up_pre.T)
    gate_grad, up_grad = run_main(
        lax.axis_index("yh").reshape(1), own.astype(jnp.float32), other.astype(jnp.float32), staged, ga, ua
    )
    return (gate_grad.T, up_grad.T, gain_grad)


def solution(mesh):
    finer = Mesh(mesh.devices.reshape(2, 4, 2, Z, 2), ALL)
    in_specs = (P(ALL, None), P(ALL, None), P(), P(MP, DP), P(DP, MP), P(DP, MP))
    out_specs = (P(DP, MP), P(DP, MP), P())
    return jax.shard_map(steps, mesh=finer, in_specs=in_specs, out_specs=out_specs, check_vma=False)
```

time: 141 us -> 133 us (0.943)
  Pallas kernels: 12.7 us -> 6.64 us
  waiting for transfers between devices: 19.7 us -> 17.5 us
  local copies, waits for them, and re-layouts: 0.91 us -> 2.97 us
  other arithmetic: 4.36 us -> 2.55 us
    pallas_call x3, Pallas kernels: 12.7 us -> 6.64 us  [the longest x1 3.55 us: run_main(): pl.pallas_call(main_kernel, grid=(NSTEP,), in_specs=[pl.BlockSpec(memory_...]
    all_to_all x1, waiting for transfers between devices: 7.17 us -> 4.58 us  [spread(): lax.all_to_all(jnp.broadcast_to(v[None], (n,) + v.shape), axes, 0, 0, til...]
    unnamed x0 -> x10, local copies, waits for them, and re-layouts: none -> 2.18 us
  transfers between devices with their start and end apart: 3 -> 3, of which waited for: 2 -> 2; matrix products, arithmetic and copies ran while one was open for 4% -> 3% of each run, Pallas kernels for 1% -> 0%
where the time goes in v1:
time: 133 us
  blocking collectives  63.2 us (48%)
  starting transfers between devices  25.8 us (19%)
  waiting for transfers between devices  17.5 us (13%)
  between operations  14.2 us (11%)
  Pallas kernels  6.64 us (5%)
  local copies, waits for them, and re-layouts  2.97 us (2%)
  other arithmetic  2.55 us (2%)
    all_gather x1, blocking collectives, steps(): got = lax.all_gather(message.astype(jnp.float16), 'z', axis=0)  63.2 us
    all_to_all x1, starting transfers between devices, spread(): lax.all_to_all(jnp.broadcast_to(v[None], (n,) + v.shape), axes, 0, 0, til...  21 us
    ppermute x1, waiting for transfers between devices, steps(): other = lax.ppermute(own, 'yh', [(0, 1), (1, 0)])  12.3 us
    ppermute x1, starting transfers between devices, steps(): other = lax.ppermute(own, 'yh', [(0, 1), (1, 0)])  4.77 us
    all_to_all x1, waiting for transfers between devices, spread(): lax.all_to_all(jnp.broadcast_to(v[None], (n,) + v.shape), axes, 0, 0, til...  4.58 us
    pallas_call x1, Pallas kernels, run_main(): pl.pallas_call(main_kernel, grid=(NSTEP,), in_specs=[pl.BlockSpec(memory_...  3.55 us
    pallas_call x1, Pallas kernels, run_factors(): pl.pallas_call(factor_kernel, in_specs=[pl.BlockSpec(memory_space=pl.ANY)...  2.68 us
  transfers between devices with their start and end apart: 3, of which 2 were waited for; matrix products, arithmetic and copies ran while one was open for 3% of the time, Pallas kernels for 0%

profile of v1, /device:TPU:1, one launch (start us, length us, event | category | flops | bytes accessed | tf_op | source)
XLA Modules:
  0.0 132.9 jit_solution(9004487554025594885)
XLA Ops:
  7.2 0.0 all-gather.4.cloned.1.call-start
  7.2 0.7 all-gather.4.cloned.1.call-update
  7.9 0.0 copy-start.2
  7.9 0.7 copy-done.2
  8.6 0.0 copy-start.3
  8.6 0.7 copy-done.3
  9.3 0.0 copy-start.4
  9.4 0.7 copy-done.4
  10.1 0.4 pre.1
  10.5 63.2 %all-gather.5 = f16[5120,128]{1,0:T(8,128)(2,1)S(1)} all-gather(f16[160,128]{1,0:T(8,128)(2,1)S(1)} %convert_element_type.20), channel_id=2, replica_groups=mesh['yl'=2,'x'=4,'c'=2,'z'=32,'yh'=2] {'z'}, dimensions={0}, use_global_device_ids=true | all-gather | bytes 1351680 | tf_op jit(solution)/shard_map/all_gather | solution.py:188
  73.7 0.2 slice_convert_fusion
  73.9 0.1 slice_reduce_fusion
  74.0 0.2 fusion.3
  74.2 0.8 broadcast_in_dim.5
  75.0 21.0 %all-to-all-start = ((f16[32,40,128]{2,1,0:T(8,128)(2,1)}), f16[32,40,128]{2,1,0:T(8,128)(2,1)S(1)}, u32[]{:S(2)}, u32[]{:S(2)}) async-start(f16[32,40,128]{2,1,0:T(8,128)(2,1)} %broadcast_in_dim.5), calls=%async_computation | async-start | bytes 655360 | tf_op jit(solution)/shard_map/all_to_all | solution.py:170
  96.1 4.8 %collective-permute-start = (f16[2560,128]{1,0:T(8,128)(2,1)S(1)}, f16[2560,128]{1,0:T(8,128)(2,1)}, u32[]{:S(2)}, u32[]{:S(2)}) collective-permute-start(f16[2560,128]{1,0:T(8,128)(2,1)S(1)} %bitcast.15), channel_id=1, source_target_pairs={{0,1},{1,0},{2,3},{3,2},{4,5},{5,4},{6,7},{7,6},{8,9},{9,8},{10,11... | collective-permute-start | bytes 1966088 | tf_op jit(solution)/shard_map/ppermute | solution.py:190
  100.8 0.1 bitcast_convert_fusion.own_ref
  101.0 4.6 %all-to-all-done = f16[32,40,128]{2,1,0:T(8,128)(2,1)S(1)} async-done(((f16[32,40,128]{2,1,0:T(8,128)(2,1)}), f16[32,40,128]{2,1,0:T(8,128)(2,1)S(1)}, u32[]{:S(2)}, u32[]{:S(2)}) %all-to-all-start) | async-done | bytes 327712 | tf_op jit(solution)/shard_map/all_to_all | solution.py:170
  105.7 0.0 copy-start
  105.7 0.0 copy-start.1
  105.7 0.7 fusion
  106.4 12.3 %collective-permute-done = f16[2560,128]{1,0:T(8,128)(2,1)} collective-permute-done((f16[2560,128]{1,0:T(8,128)(2,1)S(1)}, f16[2560,128]{1,0:T(8,128)(2,1)}, u32[]{:S(2)}, u32[]{:S(2)}) %collective-permute-start) | collective-permute-done | bytes 655392 | tf_op jit(solution)/shard_map/ppermute | solution.py:190
  118.6 1.2 convert_element_type.22.rec_ref
  119.8 0.0 all-gather.4.cloned.1.call-done.w_hbm
  119.8 0.0 copy-done
  119.8 0.0 copy-done.1
  119.8 2.7 %factors.1 = (bf16[4608,576]{1,0:T(8,128)(2,1)S(1)}, f32[576,128]{1,0:T(8,128)S(1)}, f32[576,128]{1,0:T(8,128)S(1)}) custom-call(bf16[4608,576]{1,0:T(8,128)(2,1)} %all-gather.4.cloned.1.call-done.w_hbm, bf16[576,128]{1,0:T(8,128)(2,1)S(1)} %bitcast.12, bf16[576,128]{1,0:T(8,128)(2,1)S(1)} %bitcast.13), custom_call_target="tpu_custom_call" | custom-call | flops 1474560 | bytes 11501568 | tf_op jit(solution)/shard_map/factors/pallas_call | solution.py:127
  122.5 3.5 %main.1 = (f32[576,128]{1,0:T(8,128)}, f32[576,128]{1,0:T(8,128)}) custom-call(s32[1]{0:T(128)} %bitcast.yh_ref, f32[2560,128]{1,0:T(8,128)S(1)} %bitcast_convert_fusion.own_ref, f32[2560,128]{1,0:T(8,128)S(1)} %convert_element_type.22.rec_ref, bf16[4608,576]{1,0:T(8,128)(2,1)S(1)} %get-tuple-element.8.w_ref, f32[576,128]{1,0:T(8,128)S(1)} %get-tuple-element.9.ga_ref, ...), custom_call_target="tpu_custom_call" | custom-call | tf_op jit(solution)/shard_map/main/pallas_call | solution.py:145
  (8 shorter events, 0.1 us)
Async XLA Ops:
  7.2 112.6 %all-gather.4.cloned.1.call-start = ((), (), s32[]{:S(2)}) async-start(), calls=%async_computation.1 | async-start | bytes 6266880 | tf_op jit(solution)/shard_map/all_gather | solution.py:174
  7.9 0.7 copy-start.2
  8.6 0.7 copy-start.3
  9.3 0.7 copy-start.4
  75.0 30.5 %all-to-all-start = ((f16[32,40,128]{2,1,0:T(8,128)(2,1)}), f16[32,40,128]{2,1,0:T(8,128)(2,1)S(1)}, u32[]{:S(2)}, u32[]{:S(2)}) async-start(f16[32,40,128]{2,1,0:T(8,128)(2,1)} %broadcast_in_dim.5), calls=%async_computation | async-start | bytes 655360 | tf_op jit(solution)/shard_map/all_to_all | solution.py:170
  96.1 22.5 %collective-permute-start = (f16[2560,128]{1,0:T(8,128)(2,1)S(1)}, f16[2560,128]{1,0:T(8,128)(2,1)}, u32[]{:S(2)}, u32[]{:S(2)}) collective-permute-start(f16[2560,128]{1,0:T(8,128)(2,1)S(1)} %bitcast.15), channel_id=1, source_target_pairs={{0,1},{1,0},{2,3},{3,2},{4,5},{5,4},{6,7},{7,6},{8,9},{9,8},{10,11... | collective-permute-start | bytes 1966088 | tf_op jit(solution)/shard_map/ppermute | solution.py:190
  105.7 14.2 %copy-start = (bf16[128,576]{0,1:T(8,128)(2,1)S(1)}, bf16[128,576]{0,1:T(8,128)(2,1)}, u32[]{:S(2)}) copy-start(bf16[128,576]{0,1:T(8,128)(2,1)} %param.10) | copy-start | bytes 442372
  105.7 14.2 %copy-start.1 = (bf16[128,576]{0,1:T(8,128)(2,1)S(1)}, bf16[128,576]{0,1:T(8,128)(2,1)}, u32[]{:S(2)}) copy-start(bf16[128,576]{0,1:T(8,128)(2,1)} %param.11) | copy-start | bytes 442372
Sparse Core Ops, SparseCore 0:
  10.7 68.1 all-gather.3
